TPU v7x, 32 devices: a whole 2x2x4 slice. The times are simulated.
32 devices in a mesh: win: 2 (over y), dx: 4 (over z), dy: 2 (over x), dz: 2 (over core).
Axes of the slice: x: 2, y: 2, z: 4, core: 2. Of those that a mesh axis runs over, the one named last changes fastest.
Arguments:
- fraction: float32 [3, 8, 2, 2, 768], P(None, ('win', 'dx'), 'dy', 'dz'), parts along dimension 1, may hold values from 0 to 1
- atom_type: int32 [8, 2, 2, 768], P(('win', 'dx'), 'dy', 'dz'), parts along dimension 0, may hold values from 0 to 31
- perturbed: int32 [8, 2, 2, 768], P(('win', 'dx'), 'dy', 'dz'), parts along dimension 0, may hold values from 0 to 1
- leaving: int32 [8, 2, 2, 2, 16], P(('win', 'dx'), 'dy', 'dz'), parts along dimension 0, may hold values from 0 to 767, as said below
- neighbours: int32 [8, 2, 2, 6, 16], P(('win', 'dx'), 'dy', 'dz'), parts along dimension 0, may hold values from 0 to 161, as said below
- counts: int32 [8, 2, 2, 6], P(('win', 'dx'), 'dy', 'dz'), parts along dimension 0, may hold values from 1 to 16, as said below
- sigma_table: float32 [32], replicated, may hold values from 0.8 to 1.2
- depth_table: float32 [32], replicated, may hold values from 0.002 to 0.03
- charge_table: float32 [32], replicated, may hold values from -1 to 1
- domain_edge: float32 [3], replicated, may hold values from 1 to 1.12
- coupling: float32 [2], P('win'), parts along dimension 0, may hold values from 0.1 to 0.9
Outputs:
- forces: float32 [3, 8, 2, 2, 768], P(None, ('win', 'dx'), 'dy', 'dz'), parts along dimension 1
- energy: float32 [2], P('win'), parts along dimension 0
- dhdl: float32 [2], P('win'), parts along dimension 0
There are 2 independent parts, one for each index of `win`. A program takes and returns all parts, laid end to end along the dimension named above; an argument that names none is the same for every part. Nothing has to cross between parts.
Inputs may be any that keep to these rules, and one draw needn't show every extreme that they name: `leaving`: each domain lists 2 * 16 distinct slots: the first 16 leave toward the next domain, the last 16 toward the previous one. `neighbours`: each list holds 16 distinct ghost block numbers; entries at or past the block's count are valid numbers and are not used. `counts`: some block lists exactly 16 blocks in every draw.
All inputs are finite; a program needn't handle non-finite values.
Results may differ from a plain program's by a relative error of at most 0.0003.
Values sent between devices are 32-bit elements; how exact they have to be, the bound alone decides.
A program may use at most 64 MiB of HBM per device.

v0:
```python
import jax
import jax.numpy as jnp
from jax import lax
from jax.sharding import PartitionSpec as P

soft_base = 0.3
soft_alpha = 0.5
charge_base = 0.3
charge_alpha = 0.5
coulomb = 0.1


def passed_along(array, axis, by):
    devices = lax.axis_size(axis)
    return lax.ppermute(array, axis, [(i, (i + by) % devices) for i in range(devices)])


def extended(block, sides, width):
    for axis, dim in sides:
        count = lax.axis_size(axis)
        forward = [(i, i + 1) for i in range(count - 1)]
        forward.append((count - 1, 0))
        backward = [(target, source) for source, target in forward]
        low = lax.ppermute(
            lax.slice_in_dim(block, block.shape[dim] - width, None, axis=dim), axis, forward
        )
        high = lax.ppermute(lax.slice_in_dim(block, 0, width, axis=dim), axis, backward)
        block = jnp.concatenate([low, block, high], axis=dim)
    return block


def swapped(block, axis, bit):
    count = lax.axis_size(axis)
    route = []
    for low in range(count):
        high = low | 1 << bit
        if high != low and high < count:
            route += [(low, high), (high, low)]
    return lax.ppermute(block, axis, route)


def lookup(table_row, type_ids):
    onehot = type_ids[None, :] == jnp.arange(table_row.shape[0], dtype=jnp.int32)[:, None]
    return jnp.sum(jnp.where(onehot, table_row[:, None], jnp.float32(0.0)), axis=0)


def pair_block(own_block, other_blocks, live_pairs, coupling_value):
    separation = own_block[0:3][None, :, :, None] - other_blocks[:, 0:3][:, :, None, :]
    radius_sq = jnp.sum(separation * separation, axis=1)
    sigma_pair = 0.5 * (own_block[3][None, :, None] + other_blocks[:, 3][:, None, :])
    depth_pair = jnp.sqrt(own_block[4][None, :, None] * other_blocks[:, 4][:, None, :])
    charges = own_block[5][None, :, None] * other_blocks[:, 5][:, None, :]
    flagged = jnp.maximum(own_block[6][None, :, None], other_blocks[:, 6][:, None, :])
    scaled = coupling_value * flagged
    sigma_two = sigma_pair * sigma_pair
    sigma_six = sigma_two * sigma_two * sigma_two
    soft_six = sigma_six * (soft_base + soft_alpha * scaled) + radius_sq * radius_sq * radius_sq
    soft_two = charge_base + charge_alpha * scaled + radius_sq
    inverse_six = 1.0 / soft_six
    energy_lj = (
        4.0
        * depth_pair
        * (sigma_six * sigma_six * inverse_six * inverse_six - sigma_six * inverse_six)
    )
    grad_six = (
        4.0
        * depth_pair
        * (
            sigma_six * inverse_six * inverse_six
            - 2.0 * sigma_six * sigma_six * inverse_six * inverse_six * inverse_six
        )
    )
    energy_coul = coulomb * charges * lax.rsqrt(soft_two)
    grad_two = -0.5 * energy_coul / soft_two
    weight = 1.0 - scaled
    total_pair = energy_lj + energy_coul
    pair_energy = jnp.sum(weight * total_pair * live_pairs)
    pair_dhdl = jnp.sum(
        flagged
        * (-total_pair + weight * (grad_six * sigma_six * soft_alpha + grad_two * charge_alpha))
        * live_pairs
    )
    force_scale = -weight * (6.0 * radius_sq * radius_sq * grad_six + 2.0 * grad_two) * live_pairs
    forces = jnp.sum(force_scale[:, None] * separation, axis=(0, 3))
    return (forces, pair_energy, pair_dhdl)


def block_terms(ghost_rows, listed_blocks, list_count, block_id, block_total, coupling_value):
    centre = 13 * block_total + block_id
    own_block = lax.dynamic_index_in_dim(ghost_rows, centre, 0, keepdims=False)
    other_blocks = jnp.take(ghost_rows, listed_blocks, axis=0)
    valid_slot = (jnp.arange(listed_blocks.shape[0], dtype=jnp.int32) < list_count).astype(
        jnp.float32
    )
    is_self = (listed_blocks == centre).astype(jnp.float32)[:, None, None] * jnp.eye(
        128, dtype=jnp.float32
    )[None]
    live_pairs = valid_slot[:, None, None] * (1.0 - is_self)
    return pair_block(own_block, other_blocks, live_pairs, coupling_value)


def on_device(
    fraction,
    atom_type,
    perturbed,
    leaving,
    neighbours,
    counts,
    sigma_table,
    depth_table,
    charge_table,
    domain_edge,
    coupling,
):
    atom_count = fraction.shape[-1]
    block_total = atom_count // 128
    spacing = float(atom_count) ** (1.0 / 3.0)
    type_ids = atom_type.reshape(atom_count)
    payload = jnp.concatenate(
        [
            fraction.reshape(3, atom_count),
            lookup(sigma_table, type_ids)[None],
            lookup(depth_table, type_ids)[None],
            lookup(charge_table, type_ids)[None],
            perturbed.reshape(1, atom_count).astype(jnp.float32),
        ],
        axis=0,
    )
    leave_slots = leaving.reshape(2, -1)
    shift_x = jnp.zeros((7, 1), jnp.float32).at[0].set(1.0)
    upward = payload[:, leave_slots[0]]
    downward = payload[:, leave_slots[1]]
    from_below = passed_along(upward, "dx", 1) - shift_x
    from_above = passed_along(downward, "dx", -1) + shift_x
    moved = payload.at[:, leave_slots[1]].set(from_below).at[:, leave_slots[0]].set(from_above)
    domain_block = moved.reshape(7, 1, 1, 1, atom_count)
    ghost_plane = extended(domain_block, (("dx", 1), ("dy", 2)), 1)
    partner = swapped(ghost_plane, "dz", 0)
    ghost_cells = jnp.concatenate([partner, ghost_plane, partner], axis=3)
    image_steps = jnp.arange(3, dtype=jnp.float32) - 1.0
    position = jnp.stack(
        [
            (ghost_cells[0] + image_steps[:, None, None, None]) * domain_edge[0] * spacing,
            (ghost_cells[1] + image_steps[None, :, None, None]) * domain_edge[1] * spacing,
            (ghost_cells[2] + image_steps[None, None, :, None]) * domain_edge[2] * spacing,
        ],
        axis=0,
    )
    ghost_all = jnp.concatenate([position, ghost_cells[3:]], axis=0)
    ghost_rows = (
        ghost_all.reshape(7, 27, block_total, 128)
        .transpose(1, 2, 0, 3)
        .reshape(27 * block_total, 7, 128)
    )
    listed = neighbours.reshape(block_total, -1)
    listed_count = counts.reshape(block_total)
    coupling_value = coupling[0]

    def one_block(block_id):
        return block_terms(
            ghost_rows,
            listed[block_id],
            listed_count[block_id],
            block_id,
            block_total,
            coupling_value,
        )

    forces, energies, dhdls = lax.map(one_block, jnp.arange(block_total, dtype=jnp.int32))
    forces = forces.transpose(1, 0, 2).reshape(3, 1, 1, 1, atom_count)
    window_energy, window_dhdl = lax.psum((jnp.sum(energies), jnp.sum(dhdls)), ("dx", "dy", "dz"))
    slot_total = jnp.float32(
        atom_count * lax.axis_size("dx") * lax.axis_size("dy") * lax.axis_size("dz")
    )
    energy = (0.5 * window_energy / slot_total).reshape(1)
    dhdl = (0.5 * window_dhdl / slot_total).reshape(1)
    return (forces, energy, dhdl)


def solution(mesh):
    return jax.shard_map(
        on_device,
        mesh=mesh,
        in_specs=(
            P(None, ("win", "dx"), "dy", "dz", None),
            P(("win", "dx"), "dy", "dz", None),
            P(("win", "dx"), "dy", "dz", None),
            P(("win", "dx"), "dy", "dz", None, None),
            P(("win", "dx"), "dy", "dz", None, None),
            P(("win", "dx"), "dy", "dz", None),
            P(),
            P(),
            P(),
            P(),
            P("win"),
        ),
        out_specs=(P(None, ("win", "dx"), "dy", "dz", None), P("win"), P("win")),
        check_vma=False,
    )
```

profile of v0, /device:TPU:0, one launch (start us, length us, event | category | flops | bytes accessed | tf_op | source)
XLA Modules:
  0.0 154.2 jit_solution(11909424343959024680)
XLA Ops:
  0.6 0.8 fusion.44
  2.8 0.8 select_reduce_fusion
  5.1 3.1 %collective-permute-start = (f32[7,16]{0,1:T(8,128)S(1)}, f32[7,16]{0,1:T(8,128)S(1)}, u32[]{:S(2)}, u32[]{:S(2)}) collective-permute-start(f32[7,16]{0,1:T(8,128)S(1)} %bitcast.113), channel_id=1, source_target_pairs={{0,4},{4,8},{8,12},{12,0},{1,5},{5,9},{9,13},{13,1},{2,6},{6,10},{... | collective-permute-start | bytes 1352 | tf_op jit(solution)/shard_map/ppermute | solution.py:15
  8.8 2.1 %collective-permute-start.1 = (f32[7,16]{0,1:T(8,128)S(1)}, f32[7,16]{0,1:T(8,128)S(1)}, u32[]{:S(2)}, u32[]{:S(2)}) collective-permute-start(f32[7,16]{0,1:T(8,128)S(1)} %bitcast.112), channel_id=1, source_target_pairs={{0,12},{4,0},{8,4},{12,8},{1,13},{5,1},{9,5},{13,9},{2,14},{6,2},{... | collective-permute-start | bytes 1352 | tf_op jit(solution)/shard_map/ppermute | solution.py:15
  10.9 1.0 collective-permute-done
  11.9 0.9 scatter_custom_fusion
  12.9 0.8 scatter_custom_fusion.1
  13.7 3.5 %collective-permute-start.3 = (f32[7,1,1,1,768]{0,4,3,2,1:T(8,128)S(1)}, f32[7,1,1,1,768]{0,4,3,2,1:T(8,128)S(1)}, u32[]{:S(2)}, u32[]{:S(2)}) collective-permute-start(f32[7,1,1,1,768]{0,4,3,2,1:T(8,128)S(1)} %bitcast.97), channel_id=1, source_target_pairs={{4,0},{8,4},{12,8},{0,12},{5,1},{9,5},{13,9},{1,13},{6,2},{10,6},{... | collective-permute-start | bytes 64520 | tf_op jit(solution)/shard_map/ppermute | solution.py:27
  17.4 9.4 %collective-permute-done.3 = f32[7,1,1,1,768]{0,4,3,2,1:T(8,128)S(1)} collective-permute-done((f32[7,1,1,1,768]{0,4,3,2,1:T(8,128)S(1)}, f32[7,1,1,1,768]{0,4,3,2,1:T(8,128)S(1)}, u32[]{:S(2)}, u32[]{:S(2)}) %collective-permute-start.3) | collective-permute-done | bytes 21536 | tf_op jit(solution)/shard_map/ppermute | solution.py:27
  26.9 6.7 %collective-permute-done.2 = f32[7,1,1,1,768]{0,4,3,2,1:T(8,128)S(1)} collective-permute-done((f32[7,1,1,1,768]{0,4,3,2,1:T(8,128)S(1)}, f32[7,1,1,1,768]{0,4,3,2,1:T(8,128)S(1)}, u32[]{:S(2)}, u32[]{:S(2)}) %collective-permute-start.2) | collective-permute-done | bytes 21536 | tf_op jit(solution)/shard_map/ppermute | solution.py:24
  33.9 1.6 %collective-permute-start.5 = (f32[7,3,1,1,768]{4,3,2,1,0:T(1,128)S(1)}, f32[7,3,1,1,768]{4,3,2,1,0:T(1,128)S(1)}, u32[]{:S(2)}, u32[]{:S(2)}) collective-permute-start(f32[7,3,1,1,768]{4,3,2,1,0:T(1,128)S(1)} %pad_maximum_fusion.2), channel_id=1, source_target_pairs={{2,0},{0,2},{3,1},{1,3},{6,4},{4,6},{7,5},{5,7},{10,8},{8,10},{11,... | collective-permute-start | bytes 193544 | tf_op jit(solution)/shard_map/ppermute | solution.py:27
  36.0 2.2 %collective-permute-done.5 = f32[7,3,1,1,768]{4,3,2,1,0:T(1,128)S(1)} collective-permute-done((f32[7,3,1,1,768]{4,3,2,1,0:T(1,128)S(1)}, f32[7,3,1,1,768]{4,3,2,1,0:T(1,128)S(1)}, u32[]{:S(2)}, u32[]{:S(2)}) %collective-permute-start.5) | collective-permute-done | bytes 64544 | tf_op jit(solution)/shard_map/ppermute | solution.py:27
  38.2 1.5 collective-permute-done.4
  41.5 2.3 %fusion.34 = (f32[1,3,3,3,768]{4,0,3,2,1:T(1,128)S(1)}, f32[1,3,3,3,768]{4,0,3,2,1:T(1,128)S(1)}, f32[1,3,3,3,768]{4,0,3,2,1:T(1,128)S(1)}) fusion(f32[7,3,3,3,768]{4,0,3,2,1:T(8,128)S(1)} %copy_dynamic-update-slice_fusion.1, f32[3]{0:T(128)S(1)} %iota_add_fusion, f32[]{:T(128)} %bitcast.28, f32[]{:T(128)} %bitcast.32, f32[]{:T(128)} %bitcast.30), kind=kLoop, calls=%fused_computation.81 | loop fusion | flops 186624 | bytes 499212 | tf_op jit(solution)/shard_map/mul | solution.py:143
  44.2 72.7 %while.17 = (s32[]{:T(128)}, f32[6,3,128]{2,1,0:T(4,128)S(1)}, f32[6]{0:T(128)S(1)}, f32[6]{0:T(128)S(1)}, f32[]{:T(128)}, /*index=5*/s32[6]{0:T(128)S(1)}, f32[...) while((s32[]{:T(128)}, f32[6,3,128]{2,1,0:T(4,128)S(1)}, ...), condition=%wide.region_10.11_spmd, body=%wide.region_5.10_spmd.sunk | while | flops 20495192 | bytes 4781457 | solution.py:169
  50.5 3.8 %fusion.57 = (f32[]{:T(128)}, f32[]{:T(128)}, f32[16,128,128]{2,1,0:T(8,128)S(1)}) fusion(f32[128,128]{1,0:T(8,128)S(1)} %fusion.53, f32[16]{0:T(128)S(1)} %get-tuple-element.249, f32[16]{0:T(128)S(1)} %get-tuple-element.250, f32[16,128]{1,0:T(8,128)S(1)} %bitcast.104, f32[128]{0:T(128)S(1)} %get-tuple-element.253, f32[16,128]{1,0:T(8,128)S(1)} %bitcast.105, ...), kind=kLoop, calls=%fused_computation.33.clone.1 | loop fusion | flops 15990782 | bytes 2197644 | tf_op jit(solution)/shard_map/while/body/eval_jaxpr/reduce_sum | solution.py:78
  54.8 0.8 dynamic_update_slice.25
  62.6 3.8 %fusion.57 = (f32[]{:T(128)}, f32[]{:T(128)}, f32[16,128,128]{2,1,0:T(8,128)S(1)}) fusion(f32[128,128]{1,0:T(8,128)S(1)} %fusion.53, f32[16]{0:T(128)S(1)} %get-tuple-element.249, f32[16]{0:T(128)S(1)} %get-tuple-element.250, f32[16,128]{1,0:T(8,128)S(1)} %bitcast.104, f32[128]{0:T(128)S(1)} %get-tuple-element.253, f32[16,128]{1,0:T(8,128)S(1)} %bitcast.105, ...), kind=kLoop, calls=%fused_computation.33.clone.1 | loop fusion | flops 15990782 | bytes 2197644 | tf_op jit(solution)/shard_map/while/body/eval_jaxpr/reduce_sum | solution.py:78
  66.9 0.8 dynamic_update_slice.25
  67.7 0.8 dynamic_update_slice.26
  74.7 3.8 %fusion.57 = (f32[]{:T(128)}, f32[]{:T(128)}, f32[16,128,128]{2,1,0:T(8,128)S(1)}) fusion(f32[128,128]{1,0:T(8,128)S(1)} %fusion.53, f32[16]{0:T(128)S(1)} %get-tuple-element.249, f32[16]{0:T(128)S(1)} %get-tuple-element.250, f32[16,128]{1,0:T(8,128)S(1)} %bitcast.104, f32[128]{0:T(128)S(1)} %get-tuple-element.253, f32[16,128]{1,0:T(8,128)S(1)} %bitcast.105, ...), kind=kLoop, calls=%fused_computation.33.clone.1 | loop fusion | flops 15990782 | bytes 2197644 | tf_op jit(solution)/shard_map/while/body/eval_jaxpr/reduce_sum | solution.py:78
  79.0 0.8 dynamic_update_slice.25
  79.8 0.8 dynamic_update_slice.26
  86.8 3.8 %fusion.57 = (f32[]{:T(128)}, f32[]{:T(128)}, f32[16,128,128]{2,1,0:T(8,128)S(1)}) fusion(f32[128,128]{1,0:T(8,128)S(1)} %fusion.53, f32[16]{0:T(128)S(1)} %get-tuple-element.249, f32[16]{0:T(128)S(1)} %get-tuple-element.250, f32[16,128]{1,0:T(8,128)S(1)} %bitcast.104, f32[128]{0:T(128)S(1)} %get-tuple-element.253, f32[16,128]{1,0:T(8,128)S(1)} %bitcast.105, ...), kind=kLoop, calls=%fused_computation.33.clone.1 | loop fusion | flops 15990782 | bytes 2197644 | tf_op jit(solution)/shard_map/while/body/eval_jaxpr/reduce_sum | solution.py:78
  91.1 0.8 dynamic_update_slice.25
  98.9 3.8 %fusion.57 = (f32[]{:T(128)}, f32[]{:T(128)}, f32[16,128,128]{2,1,0:T(8,128)S(1)}) fusion(f32[128,128]{1,0:T(8,128)S(1)} %fusion.53, f32[16]{0:T(128)S(1)} %get-tuple-element.249, f32[16]{0:T(128)S(1)} %get-tuple-element.250, f32[16,128]{1,0:T(8,128)S(1)} %bitcast.104, f32[128]{0:T(128)S(1)} %get-tuple-element.253, f32[16,128]{1,0:T(8,128)S(1)} %bitcast.105, ...), kind=kLoop, calls=%fused_computation.33.clone.1 | loop fusion | flops 15990782 | bytes 2197644 | tf_op jit(solution)/shard_map/while/body/eval_jaxpr/reduce_sum | solution.py:78
  103.2 0.8 dynamic_update_slice.25
  104.0 0.8 dynamic_update_slice.26
  111.1 3.8 %fusion.57 = (f32[]{:T(128)}, f32[]{:T(128)}, f32[16,128,128]{2,1,0:T(8,128)S(1)}) fusion(f32[128,128]{1,0:T(8,128)S(1)} %fusion.53, f32[16]{0:T(128)S(1)} %get-tuple-element.249, f32[16]{0:T(128)S(1)} %get-tuple-element.250, f32[16,128]{1,0:T(8,128)S(1)} %bitcast.104, f32[128]{0:T(128)S(1)} %get-tuple-element.253, f32[16,128]{1,0:T(8,128)S(1)} %bitcast.105, ...), kind=kLoop, calls=%fused_computation.33.clone.1 | loop fusion | flops 15990782 | bytes 2197644 | tf_op jit(solution)/shard_map/while/body/eval_jaxpr/reduce_sum | solution.py:78
  115.4 0.8 dynamic_update_slice.25
  116.1 0.8 dynamic_update_slice.26
  118.7 31.8 %all-reduce = (f32[]{:T(128)}, f32[]{:T(128)}) all-reduce(f32[]{:T(128)} %reduce_sum.96, f32[]{:T(128)} %reduce_sum.97), channel_id=1, replica_groups=mesh['win'=2,'dx'=4,'dy'=2,'dz'=2] {'dx','dy','dz'}, use_global_device_ids=true, to_apply=%region_12.13 | all-reduce | flops 2 | bytes 16 | tf_op jit(solution)/shard_map/psum | solution.py:171
  (143 shorter events, 30.5 us)
Async XLA Ops:
  0.6 12.2 %copy-start.2 = (f32[7]{0:T(128)S(1)}, f32[7]{0:T(128)}, u32[]{:S(2)}) copy-start(f32[7]{0:T(128)} %constant.159.clone.1) | copy-start | bytes 88
  5.1 6.8 %collective-permute-start = (f32[7,16]{0,1:T(8,128)S(1)}, f32[7,16]{0,1:T(8,128)S(1)}, u32[]{:S(2)}, u32[]{:S(2)}) collective-permute-start(f32[7,16]{0,1:T(8,128)S(1)} %bitcast.113), channel_id=1, source_target_pairs={{0,4},{4,8},{8,12},{12,0},{1,5},{5,9},{9,13},{13,1},{2,6},{6,10},{... | collective-permute-start | bytes 1352 | tf_op jit(solution)/shard_map/ppermute | solution.py:15
  8.8 27.1 %copy-start.1 = (s32[1,1,1,6,16]{4,2,3,1,0:T(1,128)S(1)}, s32[1,1,1,6,16]{4,2,3,1,0:T(1,128)}, u32[]{:S(2)}) copy-start(s32[1,1,1,6,16]{4,2,3,1,0:T(1,128)} %param.19) | copy-start | bytes 1156
  8.8 4.0 %collective-permute-start.1 = (f32[7,16]{0,1:T(8,128)S(1)}, f32[7,16]{0,1:T(8,128)S(1)}, u32[]{:S(2)}, u32[]{:S(2)}) collective-permute-start(f32[7,16]{0,1:T(8,128)S(1)} %bitcast.112), channel_id=1, source_target_pairs={{0,12},{4,0},{8,4},{12,8},{1,13},{5,1},{9,5},{13,9},{2,14},{6,2},{... | collective-permute-start | bytes 1352 | tf_op jit(solution)/shard_map/ppermute | solution.py:15
  12.8 27.1 %copy-start = (f32[3]{0:T(128)S(1)}, f32[3]{0:T(128)}, u32[]{:S(2)}) copy-start(f32[3]{0:T(128)} %param.24) | copy-start | bytes 40
  13.7 13.0 %collective-permute-start.3 = (f32[7,1,1,1,768]{0,4,3,2,1:T(8,128)S(1)}, f32[7,1,1,1,768]{0,4,3,2,1:T(8,128)S(1)}, u32[]{:S(2)}, u32[]{:S(2)}) collective-permute-start(f32[7,1,1,1,768]{0,4,3,2,1:T(8,128)S(1)} %bitcast.97), channel_id=1, source_target_pairs={{4,0},{8,4},{12,8},{0,12},{5,1},{9,5},{13,9},{1,13},{6,2},{10,6},{... | collective-permute-start | bytes 64520 | tf_op jit(solution)/shard_map/ppermute | solution.py:27
  17.2 16.4 %collective-permute-start.2 = (f32[7,1,1,1,768]{0,4,3,2,1:T(8,128)S(1)}, f32[7,1,1,1,768]{0,4,3,2,1:T(8,128)S(1)}, u32[]{:S(2)}, u32[]{:S(2)}) collective-permute-start(f32[7,1,1,1,768]{0,4,3,2,1:T(8,128)S(1)} %bitcast.98), channel_id=1, source_target_pairs={{0,4},{4,8},{8,12},{12,0},{1,5},{5,9},{9,13},{13,1},{2,6},{6,10},{... | collective-permute-start | bytes 64520 | tf_op jit(solution)/shard_map/ppermute | solution.py:24
  33.9 4.3 %collective-permute-start.5 = (f32[7,3,1,1,768]{4,3,2,1,0:T(1,128)S(1)}, f32[7,3,1,1,768]{4,3,2,1,0:T(1,128)S(1)}, u32[]{:S(2)}, u32[]{:S(2)}) collective-permute-start(f32[7,3,1,1,768]{4,3,2,1,0:T(1,128)S(1)} %pad_maximum_fusion.2), channel_id=1, source_target_pairs={{2,0},{0,2},{3,1},{1,3},{6,4},{4,6},{7,5},{5,7},{10,8},{8,10},{11,... | collective-permute-start | bytes 193544 | tf_op jit(solution)/shard_map/ppermute | solution.py:27
  35.4 4.3 %collective-permute-start.4 = (f32[7,3,1,1,768]{4,3,2,1,0:T(1,128)S(1)}, f32[7,3,1,1,768]{4,3,2,1,0:T(1,128)S(1)}, u32[]{:S(2)}, u32[]{:S(2)}) collective-permute-start(f32[7,3,1,1,768]{4,3,2,1,0:T(1,128)S(1)} %pad_maximum_fusion.2), channel_id=1, source_target_pairs={{0,2},{2,0},{1,3},{3,1},{4,6},{6,4},{5,7},{7,5},{8,10},{10,8},{9,1... | collective-permute-start | bytes 193544 | tf_op jit(solution)/shard_map/ppermute | solution.py:24
  39.8 1.5 collective-permute-start.6
  41.5 2.7 %copy-start.3 = (s32[1,1,1,6]{3,2,1,0:T(1,128)S(1)}, s32[1,1,1,6]{3,2,1,0:T(1,128)}, u32[]{:S(2)}) copy-start(s32[1,1,1,6]{3,2,1,0:T(1,128)} %param.20) | copy-start | bytes 76
where the time goes:
time: 155 us; the launch traced here: 154 us
  other arithmetic  41.6 us (27%)
  blocking collectives  31.8 us (21%)
  local copies, waits for them, and re-layouts  23.9 us (15%)
  waiting for transfers between devices  21.5 us (14%)
  loops' own time  20 us (13%)
  starting transfers between devices  10.9 us (7%)
  between operations  4.44 us (3%)
    psum x1, blocking collectives, on_device(): lax.psum((jnp.sum(energies), jnp.sum(dhdls)), ('dx', 'dy', 'dz'))  31.8 us
    reduce_sum x6, other arithmetic, pair_block(): jnp.sum(flagged * (-total_pair + weight * (grad_six * sigma_six * soft_al...  23.1 us
    another operation x1, loops' own time, on_device(): lax.map(one_block, jnp.arange(block_total, dtype=jnp.int32))  20 us
    ppermute x2, waiting for transfers between devices, extended(): lax.ppermute(lax.slice_in_dim(block, 0, width, axis=dim), axis, backward)  11.6 us
    dynamic_update_slice x18, local copies, waits for them, and re-layouts, on_device(): lax.map(one_block, jnp.arange(block_total, dtype=jnp.int32))  9.16 us
    ppermute x2, waiting for transfers between devices, extended(): lax.ppermute(lax.slice_in_dim(block, block.shape[dim] - width, None, axis...  8.23 us
    ppermute x2, starting transfers between devices, passed_along(): lax.ppermute(array, axis, [(i, (i + by) % devices) for i in range(devices)])  5.2 us
    ppermute x2, starting transfers between devices, extended(): lax.ppermute(lax.slice_in_dim(block, 0, width, axis=dim), axis, backward)  5.1 us
  transfers between devices with their start and end apart: 7, of which 6 were waited for; matrix products, arithmetic and copies ran while one was open for 2% of the time, Pallas kernels for 0%

commit v1 on v0

v1 whole, which is shorter than its diff:
```python
import jax
import jax.numpy as jnp
from jax import lax
from jax.experimental import pallas as pl
from jax.experimental.pallas import tpu as pltpu
from jax.sharding import PartitionSpec as P

soft_base = 0.3
soft_alpha = 0.5
charge_base = 0.3
charge_alpha = 0.5
coulomb = 0.1
LANES = 128
MESH = pl.DeviceIdType.MESH
HIGHEST = lax.Precision.HIGHEST


def steps_of(count):
    return {1: (0,), 2: (0, 1)}.get(count, (-1, 0, 1))


def slot_step(step, count):
    if count == 1:
        return step * 0
    if count == 2:
        return step * step
    return step + 1


def halo_kernel(
    sizes,
    sigma_ref,
    depth_ref,
    charge_ref,
    edge_ref,
    fraction_ref,
    type_ref,
    flag_ref,
    leaving_ref,
    ghost_ref,
    outgoing,
    incoming,
    mig_send,
    mig_recv,
    send_sem,
    recv_sem,
):
    nx, ny, nz = sizes
    atoms = fraction_ref.shape[-1]
    spacing = float(atoms) ** (1.0 / 3.0)
    me = (lax.axis_index("dx"), lax.axis_index("dy"), lax.axis_index("dz"))

    def device(step):
        return {
            name: lax.rem(place + by + count, count)
            for name, place, by, count in zip(("dx", "dy", "dz"), me, step, sizes)
        }

    offsets = [(a, b, c) for a in steps_of(nx) for b in steps_of(ny) for c in steps_of(nz)]
    others = [o for o in offsets if any(o)]

    def slot(o):
        return (
            slot_step(o[0], nx) * len(steps_of(ny)) + slot_step(o[1], ny)
        ) * len(steps_of(nz)) + slot_step(o[2], nz)

    barrier = pltpu.get_barrier_semaphore()
    for o in others:
        pl.semaphore_signal(
            barrier, inc=1, device_id=device(tuple(-x for x in o)), device_id_type=MESH
        )

    own = ghost_ref.at[slot((0, 0, 0))]
    types = type_ref[0, 0]
    sigma = jnp.zeros((1, atoms), jnp.float32)
    depth = jnp.zeros((1, atoms), jnp.float32)
    charge = jnp.zeros((1, atoms), jnp.float32)
    for k in range(sigma_ref.shape[0]):
        hit = types == k
        sigma = jnp.where(hit, sigma_ref[k], sigma)
        depth = jnp.where(hit, depth_ref[k], depth)
        charge = jnp.where(hit, charge_ref[k], charge)
    edge = [edge_ref[k] * spacing for k in range(3)]
    rows = [fraction_ref[k, 0, 0] * edge[k] for k in range(3)]
    flag = flag_ref[0, 0].astype(jnp.float32)
    rows += [sigma * 0.5, jnp.sqrt(depth) * 2.0, charge, flag, flag * 0.0]
    payload = jnp.concatenate(rows, axis=0)
    leave = leaving_ref[0, 0, 0]
    mig = leave.shape[1]
    place = lax.broadcasted_iota(jnp.int32, (atoms, mig), 0)
    up_hot = (place == leave[0:1]).astype(jnp.float32)
    down_hot = (place == leave[1:2]).astype(jnp.float32)
    first = lax.broadcasted_iota(jnp.int32, (8, mig), 0) == 0
    shift = jnp.where(first, edge[0], 0.0)
    outgoing[0] = jnp.dot(payload, up_hot, precision=HIGHEST) - shift
    outgoing[1] = jnp.dot(payload, down_hot, precision=HIGHEST) + shift
    contract = (((1,), (1,)), ((), ()))
    ones = jnp.ones((8, mig), jnp.float32)
    gone = lax.dot_general(ones, up_hot + down_hot, contract, precision=HIGHEST)
    kept = jnp.where(gone > 0.5, 0.0, payload)

    pl.semaphore_wait(barrier, len(others))
    moves = []
    for side, by in ((0, 1), (1, -1)):
        move = pltpu.make_async_remote_copy(
            src_ref=outgoing.at[side],
            dst_ref=incoming.at[side],
            send_sem=mig_send.at[side],
            recv_sem=mig_recv.at[side],
            device_id=device((by, 0, 0)),
            device_id_type=MESH,
        )
        move.start()
        moves.append(move)
    for move in moves:
        move.wait()
    from_below = lax.dot_general(incoming[0], down_hot, contract, precision=HIGHEST)
    from_above = lax.dot_general(incoming[1], up_hot, contract, precision=HIGHEST)
    own[...] = kept + from_below + from_above
    copies = []
    for k, o in enumerate(sorted(others, key=lambda o: -sum(map(abs, o)))):
        copy = pltpu.make_async_remote_copy(
            src_ref=own,
            dst_ref=ghost_ref.at[slot(o)],
            send_sem=send_sem.at[k],
            recv_sem=recv_sem.at[k],
            device_id=device(tuple(-x for x in o)),
            device_id_type=MESH,
        )
        copy.start()
        copies.append(copy)
    for copy in copies:
        copy.wait()


def pair_kernel(
    sizes,
    listed_ref,
    count_ref,
    edge_ref,
    coupling_ref,
    ghost_ref,
    force_ref,
    sums_ref,
    own_cols,
    force_acc,
):
    nx, ny, nz = sizes
    atoms = ghost_ref.shape[-1]
    blocks = atoms // LANES
    spacing = float(atoms) ** (1.0 / 3.0)
    edge = [edge_ref[k] * spacing for k in range(3)]
    lam = coupling_ref[0]
    own_slot = (slot_step(0, nx) * len(steps_of(ny)) + slot_step(0, ny)) * len(
        steps_of(nz)
    ) + slot_step(0, nz)
    ones = jnp.ones((8, LANES), jnp.float32)
    for k in range(3):
        sums_ref[k] = jnp.zeros((8, LANES), jnp.float32)

    def derived(flag):
        scaled = lam * flag
        return soft_base + soft_alpha * scaled, 1.0 - scaled

    @pl.loop(0, blocks)
    def _(q):
        base = pl.multiple_of(q * LANES, LANES)
        cols = ghost_ref[own_slot, :, pl.ds(base, LANES)].T
        for r in range(7):
            own_cols[r] = jnp.broadcast_to(cols[:, r : r + 1], (LANES, LANES))
        own_cols[5] = own_cols[5] * coulomb
        soft, weight = derived(own_cols[6])
        own_cols[7] = soft
        own_cols[8] = weight
        for k in range(3):
            force_acc[k] = jnp.zeros((LANES, LANES), jnp.float32)

        @pl.loop(0, count_ref[0, 0, 0, q])
        def _(e):
            listed = listed_ref[0, 0, 0, q, e]
            image = lax.div(listed, blocks)
            start = pl.multiple_of(lax.rem(listed, blocks) * LANES, LANES)
            a = lax.div(image, 9) - 1
            b = lax.rem(lax.div(image, 3), 3) - 1
            c = lax.rem(image, 3) - 1
            where_from = (
                slot_step(a, nx) * len(steps_of(ny)) + slot_step(b, ny)
            ) * len(steps_of(nz)) + slot_step(c, nz)
            rows = []
            for r in range(7):
                row = ghost_ref[where_from, pl.ds(r, 1), pl.ds(start, LANES)]
                if r < 3:
                    row = row + (a, b, c)[r].astype(jnp.float32) * edge[r]
                rows.append(jnp.broadcast_to(row, (8, LANES)))
            xj, yj, zj, hj, ej, qj, pj = rows
            aj, wj = derived(pj)

            def terms(masked):
                tot = jnp.zeros((8, LANES), jnp.float32)
                tot_p = jnp.zeros((8, LANES), jnp.float32)
                tot_k = jnp.zeros((8, LANES), jnp.float32)
                for g in range(LANES // 8):
                    at = pl.ds(g * 8, 8)
                    dx = own_cols[0, at] - xj
                    dy = own_cols[1, at] - yj
                    dz = own_cols[2, at] - zj
                    r2 = dx * dx + dy * dy + dz * dz
                    sig = own_cols[3, at] + hj
                    s2 = sig * sig
                    s6 = s2 * s2 * s2
                    eps4 = own_cols[4, at] * ej
                    qq = own_cols[5, at] * qj
                    if masked:
                        diag = (
                            lax.broadcasted_iota(jnp.int32, (8, LANES), 0) + g * 8
                            == lax.broadcasted_iota(jnp.int32, (8, LANES), 1)
                        )
                        eps4 = jnp.where(diag, 0.0, eps4)
                        qq = jnp.where(diag, 0.0, qq)
                    p = jnp.maximum(own_cols[6, at], pj)
                    soft = jnp.maximum(own_cols[7, at], aj)
                    weight = jnp.minimum(own_cols[8, at], wj)
                    r4 = r2 * r2
                    soft6 = s6 * soft + r4 * r2
                    inv = 1.0 / soft6
                    u = lax.rsqrt(soft + r2)
                    ec = qq * u
                    half = (0.5 * ec) * (u * u)
                    t = s6 * inv
                    et = eps4 * t
                    tm = t - 1.0
                    v = et * tm + ec
                    m = et * (t + tm)
                    kk = m * t + half
                    fs = weight * (3.0 * (m * (r4 * inv)) + half)
                    tot = tot + v
                    tot_p = tot_p + p * v
                    tot_k = tot_k + p * kk
                    force_acc[0, at] += fs * dx
                    force_acc[1, at] += fs * dy
                    force_acc[2, at] += fs * dz
                sums_ref[0] += tot
                sums_ref[1] += tot_p
                sums_ref[2] += tot_k

            is_self = listed == 13 * blocks + q

            @pl.when(is_self)
            def _():
                terms(True)

            @pl.when(jnp.logical_not(is_self))
            def _():
                terms(False)

        for k in range(3):
            total = lax.dot_general(
                ones, force_acc[k], (((1,), (1,)), ((), ())), precision=HIGHEST
            )
            force_ref[k, 0, 0, :, pl.ds(base, LANES)] = 2.0 * total[0:1]


def sum_kernel(sizes, atoms, coupling_ref, sums_ref, energy_ref, dhdl_ref, tile, gathered, send_sem, recv_sem):
    nx, ny, nz = sizes
    total = nx * ny * nz
    me = (lax.axis_index("dx") * ny + lax.axis_index("dy")) * nz + lax.axis_index("dz")

    def device(k):
        return {"dx": k // (ny * nz), "dy": k // nz % ny, "dz": k % nz}

    barrier = pltpu.get_barrier_semaphore()

    @pl.loop(1, total)
    def _(by):
        pl.semaphore_signal(
            barrier, inc=1, device_id=device(lax.rem(me + by, total)), device_id_type=MESH
        )

    rows = [jnp.sum(sums_ref[k], axis=0, keepdims=True) for k in range(3)]
    rows.append(jnp.zeros((5, LANES), jnp.float32))
    tile[...] = jnp.concatenate(rows, axis=0)
    gathered[me] = tile[...]
    pl.semaphore_wait(barrier, total - 1)

    def copy(by):
        return pltpu.make_async_remote_copy(
            src_ref=tile,
            dst_ref=gathered.at[me],
            send_sem=send_sem.at[by],
            recv_sem=recv_sem.at[by],
            device_id=device(lax.rem(me + by, total)),
            device_id_type=MESH,
        )

    @pl.loop(1, total)
    def _(by):
        copy(by).start()

    @pl.loop(1, total)
    def _(by):
        copy(by).wait()

    summed = jnp.sum(gathered[...], axis=0)
    whole = [jnp.sum(summed[k : k + 1]) for k in range(3)]
    lam = coupling_ref[0]
    scale = 0.5 / float(atoms * total)
    energy_ref[0] = scale * (whole[0] - lam * whole[1])
    dhdl_ref[0] = -scale * (whole[1] + (0.5 * (1.0 - lam)) * whole[2])


def on_device(sizes, fraction, atom_type, perturbed, leaving, neighbours, counts,
              sigma_table, depth_table, charge_table, domain_edge, coupling):
    nx, ny, nz = sizes
    atoms = fraction.shape[-1]
    mig = leaving.shape[-1]
    slots = len(steps_of(nx)) * len(steps_of(ny)) * len(steps_of(nz))
    smem = pl.BlockSpec(memory_space=pltpu.SMEM)
    vmem = pl.BlockSpec(memory_space=pltpu.VMEM)
    f32 = jnp.float32

    def bound(kernel, *values):
        return lambda *refs: kernel(*values, *refs)

    ghosts = pl.pallas_call(
        bound(halo_kernel, sizes),
        name="halo",
        out_shape=jax.ShapeDtypeStruct((slots, 8, atoms), f32),
        in_specs=[smem] * 4 + [vmem] * 4,
        out_specs=vmem,
        scratch_shapes=[
            pltpu.VMEM((2, 8, mig), f32),
            pltpu.VMEM((2, 8, mig), f32),
            pltpu.SemaphoreType.DMA((2,)),
            pltpu.SemaphoreType.DMA((2,)),
            pltpu.SemaphoreType.DMA((slots,)),
            pltpu.SemaphoreType.DMA((slots,)),
        ],
        compiler_params=pltpu.CompilerParams(collective_id=0, has_side_effects=True),
    )(sigma_table, depth_table, charge_table, domain_edge, fraction, atom_type, perturbed, leaving)
    forces, sums = pl.pallas_call(
        bound(pair_kernel, sizes),
        name="pairs",
        out_shape=(
            jax.ShapeDtypeStruct(fraction.shape, f32),
            jax.ShapeDtypeStruct((3, 8, LANES), f32),
        ),
        in_specs=[smem] * 4 + [vmem],
        out_specs=(vmem, vmem),
        scratch_shapes=[
            pltpu.VMEM((9, LANES, LANES), f32),
            pltpu.VMEM((3, LANES, LANES), f32),
        ],
    )(neighbours, counts, domain_edge, coupling, ghosts)
    total = nx * ny * nz
    energy, dhdl = pl.pallas_call(
        bound(sum_kernel, sizes, atoms),
        name="window_sum",
        out_shape=(jax.ShapeDtypeStruct((1,), f32), jax.ShapeDtypeStruct((1,), f32)),
        in_specs=[smem, vmem],
        out_specs=(smem, smem),
        scratch_shapes=[
            pltpu.VMEM((8, LANES), f32),
            pltpu.VMEM((total, 8, LANES), f32),
            pltpu.SemaphoreType.DMA((total,)),
            pltpu.SemaphoreType.DMA((total,)),
        ],
        compiler_params=pltpu.CompilerParams(collective_id=1, has_side_effects=True),
    )(coupling, sums)
    return forces, energy, dhdl


def solution(mesh):
    sizes = (mesh.shape["dx"], mesh.shape["dy"], mesh.shape["dz"])
    return jax.shard_map(
        lambda *arrays: on_device(sizes, *arrays),
        mesh=mesh,
        in_specs=(
            P(None, ("win", "dx"), "dy", "dz", None),
            P(("win", "dx"), "dy", "dz", None),
            P(("win", "dx"), "dy", "dz", None),
            P(("win", "dx"), "dy", "dz", None, None),
            P(("win", "dx"), "dy", "dz", None, None),
            P(("win", "dx"), "dy", "dz", None),
            P(),
            P(),
            P(),
            P(),
            P("win"),
        ),
        out_specs=(P(None, ("win", "dx"), "dy", "dz", None), P("win"), P("win")),
        check_vma=False,
    )
```

time: 155 us -> 48.4 us (0.31)
  Pallas kernels: 0 us -> 41.6 us
  other arithmetic: 41.6 us -> 0 us
  blocking collectives: 31.8 us -> 0 us
  local copies, waits for them, and re-layouts: 23.9 us -> 1.28 us
  waiting for transfers between devices: 21.5 us -> 0 us
  loops' own time: 20 us -> 0 us
  starting transfers between devices: 10.9 us -> 0 us
    pallas_call x0 -> x3, Pallas kernels: none -> 41.6 us  [the longest x1 18.3 us: on_device(): pl.pallas_call(bound(halo_kernel, sizes), name='halo', out_shape=jax.Shap...]
    psum x1 -> x0, blocking collectives: 31.8 us -> none  [on_device(): lax.psum((jnp.sum(energies), jnp.sum(dhdls)), ('dx', 'dy', 'dz'))]
    reduce_sum x21 -> x0, other arithmetic: 30.2 us -> none  [the longest x6 23.1 us: pair_block(): jnp.sum(flagged * (-total_pair + weight * (grad_six * sigma_six * soft_al...]
    ppermute x7 -> x0, waiting for transfers between devices: 21.5 us -> none  [the longest x2 11.6 us: extended(): lax.ppermute(lax.slice_in_dim(block, 0, width, axis=dim), axis, backward)]
    another operation x1 -> x0, loops' own time: 20 us -> none  [on_device(): lax.map(one_block, jnp.arange(block_total, dtype=jnp.int32))]
    ppermute x7 -> x0, starting transfers between devices: 10.9 us -> none  [the longest x2 5.2 us: passed_along(): lax.ppermute(array, axis, [(i, (i + by) % devices) for i in range(devices)])]
    dynamic_update_slice x18 -> x0, local copies, waits for them, and re-layouts: 9.16 us -> none  [on_device(): lax.map(one_block, jnp.arange(block_total, dtype=jnp.int32))]
    dynamic_slice x18 -> x0, local copies, waits for them, and re-layouts: 7.08 us -> none  [the longest x6 3.52 us: one_block(): listed_count[block_id]]
  transfers between devices with their start and end apart: 7 -> 0, of which waited for: 6 -> 0; matrix products, arithmetic and copies ran while one was open for 2% -> 0% of each run, Pallas kernels for 0% -> 0%
where the time goes in v1:
time: 48.4 us; the launch traced here: 47.7 us
  Pallas kernels  41.6 us (86%)
  between operations  4.81 us (10%)
  local copies, waits for them, and re-layouts  1.28 us (3%)
    pallas_call x1, Pallas kernels, on_device(): pl.pallas_call(bound(halo_kernel, sizes), name='halo', out_shape=jax.Shap...  18.3 us
    pallas_call x1, Pallas kernels, on_device(): pl.pallas_call(bound(pair_kernel, sizes), name='pairs', out_shape=(jax.Sh...  14 us
    pallas_call x1, Pallas kernels, on_device(): pl.pallas_call(bound(sum_kernel, sizes, atoms), name='window_sum', out_sh...  9.37 us
    unnamed x1, local copies, waits for them, and re-layouts  1.28 us

profile of v1, /device:TPU:0, one launch (start us, length us, event | category | flops | bytes accessed | tf_op | source)
XLA Modules:
  0.0 47.7 jit_solution(2986080466332732689)
XLA Ops:
  1.3 1.3 %copy.14.refs_0_ = s32[1,1,1,6,16]{4,3,2,1,0:T(8,128)} copy(s32[1,1,1,6,16]{4,2,3,1,0:T(1,128)} %param.15) | data formatting | bytes 768 | tf_op args[4]
  2.6 18.3 %halo.1.refs_4_ = f32[12,8,768]{2,1,0:T(8,128)} custom-call(f32[32]{0:T(128)} %refs_0_.3, f32[32]{0:T(128)} %refs_1_.2, f32[32]{0:T(128)} %refs_2_.2, f32[3]{0:T(128)} %refs_2_.3, f32[3,1,1,1,768]{4,3,2,1,0:T(1,128)} %refs_4_.1, s32[1,1,1,768]{3,2,1,0:T(1,128)} %refs_5_.1, s32[1,1,1,768]{3,2,1,0:T(1,128)} %refs_6_.1, s32[1,1,1,2,16]{4,3,2,1,0:T(2,128)} %refs_7_.1), custom_call_target="tpu_custom_call" | custom-call | tf_op jit(solution)/shard_map/halo/pallas_call | solution.py:324
  20.8 14.0 %pairs.1 = (f32[3,1,1,1,768]{4,3,2,1,0:T(1,128)}, f32[3,8,128]{2,1,0:T(8,128)}) custom-call(s32[1,1,1,6,16]{4,3,2,1,0:T(8,128)} %copy.14.refs_0_, s32[1,1,1,6]{3,2,1,0:T(1,128)} %refs_1_.3, f32[3]{0:T(128)} %refs_2_.3, f32[1]{0:T(128)S(6)} %copy.17.refs_3_.refs_0_, f32[12,8,768]{2,1,0:T(8,128)} %halo.1.refs_4_), custom_call_target="tpu_custom_call" | custom-call | tf_op jit(solution)/shard_map/pairs/pallas_call | solution.py:340
  34.8 9.4 %window_sum.1 = (f32[1]{0:T(128)}, f32[1]{0:T(128)}) custom-call(f32[1]{0:T(128)S(6)} %copy.17.refs_3_.refs_0_, f32[3,8,128]{2,1,0:T(8,128)} %get-tuple-element.8.refs_1_), custom_call_target="tpu_custom_call" | custom-call | tf_op jit(solution)/shard_map/window_sum/pallas_call | solution.py:355

commit v2 on v1

--- a/solution.py
+++ b/solution.py
@@ -27,11 +27,19 @@
     return step + 1
 
 
+def thirds(value):
+    high = value.astype(jnp.bfloat16).astype(jnp.float32)
+    rest = value - high
+    middle = rest.astype(jnp.bfloat16).astype(jnp.float32)
+    return jnp.concatenate([high, middle, rest - middle], axis=0)
+
+
+def joined(value):
+    return value[0:8] + value[8:16] + value[16:24]
+
+
 def halo_kernel(
     sizes,
-    sigma_ref,
-    depth_ref,
-    charge_ref,
     edge_ref,
     fraction_ref,
     type_ref,
@@ -71,39 +79,40 @@
         )
 
     own = ghost_ref.at[slot((0, 0, 0))]
-    types = type_ref[0, 0]
-    sigma = jnp.zeros((1, atoms), jnp.float32)
-    depth = jnp.zeros((1, atoms), jnp.float32)
-    charge = jnp.zeros((1, atoms), jnp.float32)
-    for k in range(sigma_ref.shape[0]):
-        hit = types == k
-        sigma = jnp.where(hit, sigma_ref[k], sigma)
-        depth = jnp.where(hit, depth_ref[k], depth)
-        charge = jnp.where(hit, charge_ref[k], charge)
     edge = [edge_ref[k] * spacing for k in range(3)]
     rows = [fraction_ref[k, 0, 0] * edge[k] for k in range(3)]
-    flag = flag_ref[0, 0].astype(jnp.float32)
-    rows += [sigma * 0.5, jnp.sqrt(depth) * 2.0, charge, flag, flag * 0.0]
-    payload = jnp.concatenate(rows, axis=0)
+    rows += [type_ref[0, 0].astype(jnp.float32), flag_ref[0, 0].astype(jnp.float32)]
+    payload = jnp.concatenate(rows + [jnp.zeros((3, atoms), jnp.float32)], axis=0)
     leave = leaving_ref[0, 0, 0]
     mig = leave.shape[1]
-    place = lax.broadcasted_iota(jnp.int32, (atoms, mig), 0)
-    up_hot = (place == leave[0:1]).astype(jnp.float32)
-    down_hot = (place == leave[1:2]).astype(jnp.float32)
-    first = lax.broadcasted_iota(jnp.int32, (8, mig), 0) == 0
-    shift = jnp.where(first, edge[0], 0.0)
-    outgoing[0] = jnp.dot(payload, up_hot, precision=HIGHEST) - shift
-    outgoing[1] = jnp.dot(payload, down_hot, precision=HIGHEST) + shift
-    contract = (((1,), (1,)), ((), ()))
-    ones = jnp.ones((8, mig), jnp.float32)
-    gone = lax.dot_general(ones, up_hot + down_hot, contract, precision=HIGHEST)
-    kept = jnp.where(gone > 0.5, 0.0, payload)
+    slots_in = jnp.concatenate([leave[0:1], leave[1:2]], axis=1)
+    slots_out = jnp.concatenate([leave[1:2], leave[0:1]], axis=1)
+    place = lax.broadcasted_iota(jnp.int32, (atoms, 2 * mig), 0)
+    hot_in = (place == slots_in).astype(jnp.float32).astype(jnp.bfloat16)
+    hot_out = (place == slots_out).astype(jnp.float32).astype(jnp.bfloat16)
+    lane = lax.broadcasted_iota(jnp.int32, (8, 2 * mig), 1)
+    first = lax.broadcasted_iota(jnp.int32, (8, 2 * mig), 0) == 0
+    shift = jnp.where(first, jnp.where(lane < mig, edge[0], -edge[0]), 0.0)
+    leavers = joined(
+        jnp.dot(thirds(payload).astype(jnp.bfloat16), hot_out, preferred_element_type=jnp.float32)
+    )
+    outgoing[...] = leavers + shift
+
+    def spread(value):
+        return lax.dot_general(
+            value.astype(jnp.bfloat16),
+            hot_in,
+            (((1,), (1,)), ((), ())),
+            preferred_element_type=jnp.float32,
+        )
+
+    gone = spread(jnp.ones((8, 2 * mig), jnp.float32))
 
     pl.semaphore_wait(barrier, len(others))
     moves = []
     for side, by in ((0, 1), (1, -1)):
         move = pltpu.make_async_remote_copy(
-            src_ref=outgoing.at[side],
+            src_ref=outgoing,
             dst_ref=incoming.at[side],
             send_sem=mig_send.at[side],
             recv_sem=mig_recv.at[side],
@@ -114,9 +123,10 @@
         moves.append(move)
     for move in moves:
         move.wait()
-    from_below = lax.dot_general(incoming[0], down_hot, contract, precision=HIGHEST)
-    from_above = lax.dot_general(incoming[1], up_hot, contract, precision=HIGHEST)
-    own[...] = kept + from_below + from_above
+    merged = jnp.where(lane < mig, incoming[1], incoming[0])
+    moved = jnp.where(gone > 0.5, joined(spread(thirds(merged))), payload)
+    for r in range(5):
+        own[r] = moved[r : r + 1]
     copies = []
     for k, o in enumerate(sorted(others, key=lambda o: -sum(map(abs, o)))):
         copy = pltpu.make_async_remote_copy(
@@ -139,11 +149,15 @@
     count_ref,
     edge_ref,
     coupling_ref,
+    sigma_ref,
+    depth_ref,
+    charge_ref,
     ghost_ref,
     force_ref,
     sums_ref,
     own_cols,
     force_acc,
+    params,
 ):
     nx, ny, nz = sizes
     atoms = ghost_ref.shape[-1]
@@ -154,30 +168,51 @@
     own_slot = (slot_step(0, nx) * len(steps_of(ny)) + slot_step(0, ny)) * len(
         steps_of(nz)
     ) + slot_step(0, nz)
-    ones = jnp.ones((8, LANES), jnp.float32)
+    ones = jnp.ones((8, LANES), jnp.bfloat16)
     for k in range(3):
         sums_ref[k] = jnp.zeros((8, LANES), jnp.float32)
 
-    def derived(flag):
-        scaled = lam * flag
-        return soft_base + soft_alpha * scaled, 1.0 - scaled
+    lane = lax.broadcasted_iota(jnp.int32, (1, LANES), 1)
+    tables = [jnp.zeros((1, LANES), jnp.float32)] * 3
+    for k in range(sigma_ref.shape[0]):
+        hit = lane == k
+        tables = [
+            jnp.where(hit, ref[k], table)
+            for ref, table in zip((sigma_ref, depth_ref, charge_ref), tables)
+        ]
+    table = jnp.concatenate(
+        [tables[0] * 0.5, jnp.sqrt(tables[1]) * 2.0, tables[2]] + [tables[2] * 0.0] * 5, axis=0
+    )
+    for place in range(ghost_ref.shape[0]):
+        for q in range(blocks):
+            span = slice(q * LANES, (q + 1) * LANES)
+            kind = ghost_ref[place, 3, :, span].astype(jnp.int32)
+            params[place, :, span] = jnp.take_along_axis(
+                table, jnp.broadcast_to(kind, (8, LANES)), axis=1, mode="promise_in_bounds"
+            )
+    picks = (
+        lax.broadcasted_iota(jnp.int32, (24, 7 * LANES), 0) % 8
+        == lax.broadcasted_iota(jnp.int32, (24, 7 * LANES), 1) // LANES
+    ).astype(jnp.float32).astype(jnp.bfloat16)
+    for q in range(blocks):
+        span = slice(q * LANES, (q + 1) * LANES)
+        known = params[own_slot, :, span]
+        rows = [ghost_ref[own_slot, r, :, span] for r in range(3)]
+        rows += [known[0:1], known[1:2], known[2:3] * coulomb]
+        rows += [ghost_ref[own_slot, 4, :, span], known[3:4]]
+        cols = thirds(jnp.concatenate(rows, axis=0)).T.astype(jnp.bfloat16)
+        wide = jnp.dot(cols, picks, preferred_element_type=jnp.float32)
+        for r in range(7):
+            own_cols[q, r] = wide[:, r * LANES : (r + 1) * LANES]
+    for q in range(blocks):
+        for k in range(3):
+            force_acc[q, k] = jnp.zeros((LANES, LANES), jnp.float32)
 
     @pl.loop(0, blocks)
     def _(q):
-        base = pl.multiple_of(q * LANES, LANES)
-        cols = ghost_ref[own_slot, :, pl.ds(base, LANES)].T
-        for r in range(7):
-            own_cols[r] = jnp.broadcast_to(cols[:, r : r + 1], (LANES, LANES))
-        own_cols[5] = own_cols[5] * coulomb
-        soft, weight = derived(own_cols[6])
-        own_cols[7] = soft
-        own_cols[8] = weight
-        for k in range(3):
-            force_acc[k] = jnp.zeros((LANES, LANES), jnp.float32)
-
         @pl.loop(0, count_ref[0, 0, 0, q])
         def _(e):
-            listed = listed_ref[0, 0, 0, q, e]
+            listed = listed_ref[q, 0, e]
             image = lax.div(listed, blocks)
             start = pl.multiple_of(lax.rem(listed, blocks) * LANES, LANES)
             a = lax.div(image, 9) - 1
@@ -188,12 +223,14 @@
             ) * len(steps_of(nz)) + slot_step(c, nz)
             rows = []
             for r in range(7):
-                row = ghost_ref[where_from, pl.ds(r, 1), pl.ds(start, LANES)]
+                if 3 <= r < 6:
+                    row = params[where_from, pl.ds(r - 3, 1), pl.ds(start, LANES)]
+                else:
+                    row = ghost_ref[where_from, min(r, 4), :, pl.ds(start, LANES)]
                 if r < 3:
                     row = row + (a, b, c)[r].astype(jnp.float32) * edge[r]
                 rows.append(jnp.broadcast_to(row, (8, LANES)))
             xj, yj, zj, hj, ej, qj, pj = rows
-            aj, wj = derived(pj)
 
             def terms(masked):
                 tot = jnp.zeros((8, LANES), jnp.float32)
@@ -201,15 +238,15 @@
                 tot_k = jnp.zeros((8, LANES), jnp.float32)
                 for g in range(LANES // 8):
                     at = pl.ds(g * 8, 8)
-                    dx = own_cols[0, at] - xj
-                    dy = own_cols[1, at] - yj
-                    dz = own_cols[2, at] - zj
+                    dx = own_cols[q, 0, at] - xj
+                    dy = own_cols[q, 1, at] - yj
+                    dz = own_cols[q, 2, at] - zj
                     r2 = dx * dx + dy * dy + dz * dz
-                    sig = own_cols[3, at] + hj
+                    sig = own_cols[q, 3, at] + hj
                     s2 = sig * sig
                     s6 = s2 * s2 * s2
-                    eps4 = own_cols[4, at] * ej
-                    qq = own_cols[5, at] * qj
+                    eps4 = own_cols[q, 4, at] * ej
+                    qq = own_cols[q, 5, at] * qj
                     if masked:
                         diag = (
                             lax.broadcasted_iota(jnp.int32, (8, LANES), 0) + g * 8
@@ -217,9 +254,9 @@
                         )
                         eps4 = jnp.where(diag, 0.0, eps4)
                         qq = jnp.where(diag, 0.0, qq)
-                    p = jnp.maximum(own_cols[6, at], pj)
-                    soft = jnp.maximum(own_cols[7, at], aj)
-                    weight = jnp.minimum(own_cols[8, at], wj)
+                    p = jnp.maximum(own_cols[q, 6, at], pj)
+                    soft = soft_base + (soft_alpha * lam) * p
+                    weight = 1.0 - lam * p
                     r4 = r2 * r2
                     soft6 = s6 * soft + r4 * r2
                     inv = 1.0 / soft6
@@ -236,9 +273,9 @@
                     tot = tot + v
                     tot_p = tot_p + p * v
                     tot_k = tot_k + p * kk
-                    force_acc[0, at] += fs * dx
-                    force_acc[1, at] += fs * dy
-                    force_acc[2, at] += fs * dz
+                    force_acc[q, 0, at] += fs * dx
+                    force_acc[q, 1, at] += fs * dy
+                    force_acc[q, 2, at] += fs * dz
                 sums_ref[0] += tot
                 sums_ref[1] += tot_p
                 sums_ref[2] += tot_k
@@ -253,11 +290,18 @@
             def _():
                 terms(False)
 
+    for q in range(blocks):
         for k in range(3):
-            total = lax.dot_general(
-                ones, force_acc[k], (((1,), (1,)), ((), ())), precision=HIGHEST
+            whole = force_acc[q, k]
+            high = whole.astype(jnp.bfloat16)
+            low = (whole - high.astype(jnp.float32)).astype(jnp.bfloat16)
+            total = sum(
+                lax.dot_general(
+                    ones, part, (((1,), (1,)), ((), ())), preferred_element_type=jnp.float32
+                )
+                for part in (high, low)
             )
-            force_ref[k, 0, 0, :, pl.ds(base, LANES)] = 2.0 * total[0:1]
+            force_ref[k, 0, 0, :, q * LANES : (q + 1) * LANES] = 2.0 * total[0:1]
 
 
 def sum_kernel(sizes, atoms, coupling_ref, sums_ref, energy_ref, dhdl_ref, tile, gathered, send_sem, recv_sem):
@@ -324,19 +368,19 @@
     ghosts = pl.pallas_call(
         bound(halo_kernel, sizes),
         name="halo",
-        out_shape=jax.ShapeDtypeStruct((slots, 8, atoms), f32),
-        in_specs=[smem] * 4 + [vmem] * 4,
+        out_shape=jax.ShapeDtypeStruct((slots, 5, 1, atoms), f32),
+        in_specs=[smem] + [vmem] * 4,
         out_specs=vmem,
         scratch_shapes=[
-            pltpu.VMEM((2, 8, mig), f32),
-            pltpu.VMEM((2, 8, mig), f32),
+            pltpu.VMEM((8, 2 * mig), f32),
+            pltpu.VMEM((2, 8, 2 * mig), f32),
             pltpu.SemaphoreType.DMA((2,)),
             pltpu.SemaphoreType.DMA((2,)),
             pltpu.SemaphoreType.DMA((slots,)),
             pltpu.SemaphoreType.DMA((slots,)),
         ],
         compiler_params=pltpu.CompilerParams(collective_id=0, has_side_effects=True),
-    )(sigma_table, depth_table, charge_table, domain_edge, fraction, atom_type, perturbed, leaving)
+    )(domain_edge, fraction, atom_type, perturbed, leaving)
     forces, sums = pl.pallas_call(
         bound(pair_kernel, sizes),
         name="pairs",
@@ -344,13 +388,14 @@
             jax.ShapeDtypeStruct(fraction.shape, f32),
             jax.ShapeDtypeStruct((3, 8, LANES), f32),
         ),
-        in_specs=[smem] * 4 + [vmem],
+        in_specs=[smem] * 7 + [vmem],
         out_specs=(vmem, vmem),
         scratch_shapes=[
-            pltpu.VMEM((9, LANES, LANES), f32),
-            pltpu.VMEM((3, LANES, LANES), f32),
+            pltpu.VMEM((atoms // LANES, 7, LANES, LANES), f32),
+            pltpu.VMEM((atoms // LANES, 3, LANES, LANES), f32),
+            pltpu.VMEM((slots, 8, atoms), f32),
         ],
-    )(neighbours, counts, domain_edge, coupling, ghosts)
+    )(neighbours.reshape(atoms // LANES, 1, -1), counts, domain_edge, coupling, sigma_table, depth_table, charge_table, ghosts)
     total = nx * ny * nz
     energy, dhdl = pl.pallas_call(
         bound(sum_kernel, sizes, atoms),

time: 48.4 us -> 43.6 us (0.901); the launches traced: 47.7 us -> 43.4 us
  Pallas kernels: 41.6 us -> 38.7 us
  local copies, waits for them, and re-layouts: 1.28 us -> 0 us
    pallas_call x1, Pallas kernels: 18.3 us -> 16.1 us  [on_device(): pl.pallas_call(bound(halo_kernel, sizes), name='halo', out_shape=jax.Shap...]
    pallas_call x1, Pallas kernels: 9.37 us -> 8.05 us  [on_device(): pl.pallas_call(bound(sum_kernel, sizes, atoms), name='window_sum', out_sh...]
    unnamed x1 -> x0, local copies, waits for them, and re-layouts: 1.28 us -> none
    pallas_call x1, Pallas kernels: 14 us -> 14.5 us  [on_device(): pl.pallas_call(bound(pair_kernel, sizes), name='pairs', out_shape=(jax.Sh...]
where the time goes in v2:
time: 43.6 us; the launch traced here: 43.4 us
  Pallas kernels  38.7 us (89%)
  between operations  4.78 us (11%)
    pallas_call x1, Pallas kernels, on_device(): pl.pallas_call(bound(halo_kernel, sizes), name='halo', out_shape=jax.Shap...  16.1 us
    pallas_call x1, Pallas kernels, on_device(): pl.pallas_call(bound(pair_kernel, sizes), name='pairs', out_shape=(jax.Sh...  14.5 us
    pallas_call x1, Pallas kernels, on_device(): pl.pallas_call(bound(sum_kernel, sizes, atoms), name='window_sum', out_sh...  8.05 us

profile of v2, /device:TPU:0, one launch (start us, length us, event | category | flops | bytes accessed | tf_op | source)
XLA Modules:
  0.0 43.4 jit_solution(3465484562044022507)
XLA Ops:
  1.3 16.1 %halo.1.refs_7_ = f32[12,5,1,768]{3,2,1,0:T(1,128)} custom-call(f32[3]{0:T(128)} %refs_2_.3, f32[3,1,1,1,768]{4,3,2,1,0:T(1,128)} %refs_1_.2, s32[1,1,1,768]{3,2,1,0:T(1,128)} %refs_2_.2, s32[1,1,1,768]{3,2,1,0:T(1,128)} %refs_3_.2, s32[1,1,1,2,16]{4,3,2,1,0:T(2,128)} %refs_4_.2), custom_call_target="tpu_custom_call" | custom-call | tf_op jit(solution)/shard_map/halo/pallas_call | solution.py:368
  17.4 14.5 %pairs.1 = (f32[3,1,1,1,768]{4,3,2,1,0:T(1,128)}, f32[3,8,128]{2,1,0:T(8,128)}) custom-call(s32[6,1,16]{2,1,0:T(1,128)} %bitcast.1, s32[1,1,1,6]{3,2,1,0:T(1,128)} %refs_1_.3, f32[3]{0:T(128)} %refs_2_.3, f32[1]{0:T(128)S(6)} %copy.16.refs_3_.refs_0_, f32[32]{0:T(128)} %refs_4_.3, f32[32]{0:T(128)} %refs_5_.1, f32[32]{0:T(128)} %refs_6_.1, ...), custom_call_target="tpu_custom_call" | custom-call | tf_op jit(solution)/shard_map/pairs/pallas_call | solution.py:384
  31.9 8.0 %window_sum.1 = (f32[1]{0:T(128)}, f32[1]{0:T(128)}) custom-call(f32[1]{0:T(128)S(6)} %copy.16.refs_3_.refs_0_, f32[3,8,128]{2,1,0:T(8,128)} %get-tuple-element.8.refs_1_), custom_call_target="tpu_custom_call" | custom-call | tf_op jit(solution)/shard_map/window_sum/pallas_call | solution.py:400

commit v3 on v2

v3 whole, which is shorter than its diff:
```python
import jax
import jax.numpy as jnp
from jax import lax
from jax.experimental import pallas as pl
from jax.experimental.pallas import tpu as pltpu
from jax.sharding import PartitionSpec as P

soft_base = 0.3
soft_alpha = 0.5
charge_base = 0.3
charge_alpha = 0.5
coulomb = 0.1
LANES = 128
MESH = pl.DeviceIdType.MESH
HIGHEST = lax.Precision.HIGHEST


def steps_of(count):
    return {1: (0,), 2: (0, 1)}.get(count, (-1, 0, 1))


def slot_step(step, count):
    if count == 1:
        return step * 0
    if count == 2:
        return step * step
    return step + 1


def thirds(value):
    high = value.astype(jnp.bfloat16).astype(jnp.float32)
    rest = value - high
    middle = rest.astype(jnp.bfloat16).astype(jnp.float32)
    return jnp.concatenate([high, middle, rest - middle], axis=0)


def joined(value):
    return value[0:8] + value[8:16] + value[16:24]


def step_kernel(
    sizes,
    edge_ref,
    coupling_ref,
    sigma_ref,
    depth_ref,
    charge_ref,
    listed_ref,
    count_ref,
    fraction_ref,
    type_ref,
    flag_ref,
    leaving_ref,
    force_ref,
    energy_ref,
    dhdl_ref,
    ghost_ref,
    outgoing,
    incoming,
    own_cols,
    force_acc,
    params,
    sums_ref,
    tile,
    gathered,
    mig_send,
    mig_recv,
    send_sem,
    recv_sem,
    sum_send,
    sum_recv,
):
    nx, ny, nz = sizes
    atoms = fraction_ref.shape[-1]
    spacing = float(atoms) ** (1.0 / 3.0)
    me = (lax.axis_index("dx"), lax.axis_index("dy"), lax.axis_index("dz"))

    def device(step):
        return {
            name: lax.rem(place + by + count, count)
            for name, place, by, count in zip(("dx", "dy", "dz"), me, step, sizes)
        }

    offsets = [(a, b, c) for a in steps_of(nx) for b in steps_of(ny) for c in steps_of(nz)]
    others = [o for o in offsets if any(o)]

    def slot(o):
        return (
            slot_step(o[0], nx) * len(steps_of(ny)) + slot_step(o[1], ny)
        ) * len(steps_of(nz)) + slot_step(o[2], nz)

    barrier = pltpu.get_barrier_semaphore()
    total = nx * ny * nz
    my_id = (me[0] * ny + me[1]) * nz + me[2]

    def window_device(k):
        return {
            "dx": lax.div(k, ny * nz),
            "dy": lax.rem(lax.div(k, nz), ny),
            "dz": lax.rem(k, nz),
        }

    @pl.loop(1, total)
    def _(by):
        pl.semaphore_signal(
            barrier,
            inc=1,
            device_id=window_device(lax.rem(my_id + by, total)),
            device_id_type=MESH,
        )

    own = ghost_ref.at[slot((0, 0, 0))]
    edge = [edge_ref[k] * spacing for k in range(3)]
    rows = [fraction_ref[k, 0, 0] * edge[k] for k in range(3)]
    rows += [type_ref[0, 0].astype(jnp.float32), flag_ref[0, 0].astype(jnp.float32)]
    payload = jnp.concatenate(rows + [jnp.zeros((3, atoms), jnp.float32)], axis=0)
    leave = leaving_ref[0, 0, 0]
    mig = leave.shape[1]
    slots_in = jnp.concatenate([leave[0:1], leave[1:2]], axis=1)
    slots_out = jnp.concatenate([leave[1:2], leave[0:1]], axis=1)
    place = lax.broadcasted_iota(jnp.int32, (atoms, 2 * mig), 0)
    hot_in = (place == slots_in).astype(jnp.float32).astype(jnp.bfloat16)
    hot_out = (place == slots_out).astype(jnp.float32).astype(jnp.bfloat16)
    lane = lax.broadcasted_iota(jnp.int32, (8, 2 * mig), 1)
    first = lax.broadcasted_iota(jnp.int32, (8, 2 * mig), 0) == 0
    shift = jnp.where(first, jnp.where(lane < mig, edge[0], -edge[0]), 0.0)
    leavers = joined(
        jnp.dot(thirds(payload).astype(jnp.bfloat16), hot_out, preferred_element_type=jnp.float32)
    )
    outgoing[...] = leavers + shift

    def spread(value):
        return lax.dot_general(
            value.astype(jnp.bfloat16),
            hot_in,
            (((1,), (1,)), ((), ())),
            preferred_element_type=jnp.float32,
        )

    gone = spread(jnp.ones((8, 2 * mig), jnp.float32))

    pl.semaphore_wait(barrier, total - 1)
    moves = []
    for side, by in ((0, 1), (1, -1)):
        move = pltpu.make_async_remote_copy(
            src_ref=outgoing,
            dst_ref=incoming.at[side],
            send_sem=mig_send.at[side],
            recv_sem=mig_recv.at[side],
            device_id=device((by, 0, 0)),
            device_id_type=MESH,
        )
        move.start()
        moves.append(move)
    for move in moves:
        move.wait()
    merged = jnp.where(lane < mig, incoming[1], incoming[0])
    moved = jnp.where(gone > 0.5, joined(spread(thirds(merged))), payload)
    for r in range(5):
        own[r] = moved[r : r + 1]
    copies = []
    for k, o in enumerate(sorted(others, key=lambda o: -sum(map(abs, o)))):
        copy = pltpu.make_async_remote_copy(
            src_ref=own,
            dst_ref=ghost_ref.at[slot(o)],
            send_sem=send_sem.at[k],
            recv_sem=recv_sem.at[k],
            device_id=device(tuple(-x for x in o)),
            device_id_type=MESH,
        )
        copy.start()
        copies.append((copy, slot(o)))

    blocks = atoms // LANES
    lam = coupling_ref[0]
    own_slot = slot((0, 0, 0))
    ones = jnp.ones((8, LANES), jnp.bfloat16)
    for k in range(3):
        sums_ref[k] = jnp.zeros((8, LANES), jnp.float32)

    ahead = lax.broadcasted_iota(jnp.int32, (8, LANES), 1) - lax.broadcasted_iota(
        jnp.int32, (8, LANES), 0
    )
    lane = lax.broadcasted_iota(jnp.int32, (1, LANES), 1)
    tables = [jnp.zeros((1, LANES), jnp.float32)] * 3
    for k in range(sigma_ref.shape[0]):
        hit = lane == k
        tables = [
            jnp.where(hit, ref[k], table)
            for ref, table in zip((sigma_ref, depth_ref, charge_ref), tables)
        ]
    table = jnp.concatenate(
        [tables[0] * 0.5, jnp.sqrt(tables[1]) * 2.0, tables[2]] + [tables[2] * 0.0] * 5, axis=0
    )
    kinds = sigma_ref.shape[0]
    table_parts = thirds(table[:, :kinds]).astype(jnp.bfloat16)
    kind_row = lax.broadcasted_iota(jnp.int32, (kinds, atoms), 0).astype(jnp.float32)

    def look_up(place):
        onehot = (kind_row == ghost_ref[place, 3]).astype(jnp.float32).astype(jnp.bfloat16)
        found = joined(jnp.dot(table_parts, onehot, preferred_element_type=jnp.float32))
        rows = [ghost_ref[place, r] for r in range(3)]
        rows += [found[0:3], ghost_ref[place, 4], found[3:4]]
        whole = jnp.concatenate(rows, axis=0)
        for q in range(blocks):
            params[place * blocks + q] = whole[:, q * LANES : (q + 1) * LANES]

    look_up(own_slot)
    picks = (
        lax.broadcasted_iota(jnp.int32, (24, 7 * LANES), 0) % 8
        == lax.broadcasted_iota(jnp.int32, (24, 7 * LANES), 1) // LANES
    ).astype(jnp.float32).astype(jnp.bfloat16)
    for q in range(blocks):
        cols = thirds(params[own_slot * blocks + q]).T.astype(jnp.bfloat16)
        wide = jnp.dot(cols, picks, preferred_element_type=jnp.float32)
        for r in range(7):
            col = wide[:, r * LANES : (r + 1) * LANES]
            own_cols[q, r] = col * coulomb if r == 5 else col
    for q in range(blocks):
        for k in range(3):
            force_acc[q, k] = jnp.zeros((LANES, LANES), jnp.float32)

    for copy, place in copies:
        copy.wait()
        look_up(place)

    @pl.loop(0, blocks)
    def _(q):
        def entry(e):
            listed = listed_ref[q, 0, e]
            left = jnp.minimum(jnp.maximum(count_ref[0, 0, 0, q] - e, 0), 1)
            used = left.astype(jnp.float32)
            apart = jnp.abs(listed - (13 * blocks + q))
            self_lane = jnp.minimum(apart, 1) * (2 * LANES)
            image = lax.div(listed, blocks)
            a = lax.div(image, 9) - 1
            b = lax.rem(lax.div(image, 3), 3) - 1
            c = lax.rem(image, 3) - 1
            where_from = (
                slot_step(a, nx) * len(steps_of(ny)) + slot_step(b, ny)
            ) * len(steps_of(nz)) + slot_step(c, nz)
            other = params[where_from * blocks + lax.rem(listed, blocks)]
            rows = []
            for r in range(7):
                row = other[r : r + 1]
                if r < 3:
                    row = row + (a, b, c)[r].astype(jnp.float32) * edge[r]
                if 4 <= r < 6:
                    row = row * used
                rows.append(jnp.broadcast_to(row, (8, LANES)))
            xj, yj, zj, hj, ej, qj, pj = rows

            tot = jnp.zeros((8, LANES), jnp.float32)
            tot_p = jnp.zeros((8, LANES), jnp.float32)
            tot_k = jnp.zeros((8, LANES), jnp.float32)
            for g in range(LANES // 8):
                at = pl.ds(g * 8, 8)
                dx = own_cols[q, 0, at] - xj
                dy = own_cols[q, 1, at] - yj
                dz = own_cols[q, 2, at] - zj
                r2 = dx * dx + dy * dy + dz * dz
                sig = own_cols[q, 3, at] + hj
                s2 = sig * sig
                s6 = s2 * s2 * s2
                eps4 = own_cols[q, 4, at] * ej
                qq = own_cols[q, 5, at] * qj
                diag = ahead == self_lane + g * 8
                eps4 = jnp.where(diag, 0.0, eps4)
                qq = jnp.where(diag, 0.0, qq)
                p = jnp.maximum(own_cols[q, 6, at], pj)
                soft = soft_base + (soft_alpha * lam) * p
                weight = 1.0 - lam * p
                r4 = r2 * r2
                soft6 = s6 * soft + r4 * r2
                inv = 1.0 / soft6
                u = lax.rsqrt(soft + r2)
                ec = qq * u
                half = (0.5 * ec) * (u * u)
                t = s6 * inv
                et = eps4 * t
                tm = t - 1.0
                v = et * tm + ec
                m = et * (t + tm)
                kk = m * t + half
                fs = weight * (3.0 * (m * (r4 * inv)) + half)
                tot = tot + v
                tot_p = tot_p + p * v
                tot_k = tot_k + p * kk
                force_acc[q, 0, at] += fs * dx
                force_acc[q, 1, at] += fs * dy
                force_acc[q, 2, at] += fs * dz
            sums_ref[0] += tot
            sums_ref[1] += tot_p
            sums_ref[2] += tot_k

        width = listed_ref.shape[-1]
        unroll = 2 if width % 2 == 0 else 1

        @pl.loop(0, width // unroll)
        def _(step):
            for k in range(unroll):
                entry(step * unroll + k)

    folded = [jnp.sum(sums_ref[k], axis=0, keepdims=True) for k in range(3)]
    folded.append(jnp.zeros((5, LANES), jnp.float32))
    mine = jnp.concatenate(folded, axis=0)
    tile[...] = mine
    gathered[my_id] = mine

    def share(by):
        return pltpu.make_async_remote_copy(
            src_ref=tile,
            dst_ref=gathered.at[my_id],
            send_sem=sum_send.at[by],
            recv_sem=sum_recv.at[by],
            device_id=window_device(lax.rem(my_id + by, total)),
            device_id_type=MESH,
        )

    @pl.loop(1, total)
    def _(by):
        share(by).start()

    for q in range(blocks):
        for k in range(3):
            whole = force_acc[q, k]
            high = whole.astype(jnp.bfloat16)
            low = (whole - high.astype(jnp.float32)).astype(jnp.bfloat16)
            reduced = sum(
                lax.dot_general(
                    ones, part, (((1,), (1,)), ((), ())), preferred_element_type=jnp.float32
                )
                for part in (high, low)
            )
            force_ref[k, 0, 0, :, q * LANES : (q + 1) * LANES] = 2.0 * reduced[0:1]

    @pl.loop(1, total)
    def _(by):
        share(by).wait()

    summed = jnp.sum(gathered[...], axis=0)
    parts = [jnp.sum(summed[k : k + 1]) for k in range(3)]
    scale = 0.5 / float(atoms * total)
    energy_ref[0] = scale * (parts[0] - lam * parts[1])
    dhdl_ref[0] = -scale * (parts[1] + (0.5 * (1.0 - lam)) * parts[2])


def on_device(sizes, fraction, atom_type, perturbed, leaving, neighbours, counts,
              sigma_table, depth_table, charge_table, domain_edge, coupling):
    nx, ny, nz = sizes
    atoms = fraction.shape[-1]
    mig = leaving.shape[-1]
    slots = len(steps_of(nx)) * len(steps_of(ny)) * len(steps_of(nz))
    smem = pl.BlockSpec(memory_space=pltpu.SMEM)
    vmem = pl.BlockSpec(memory_space=pltpu.VMEM)
    f32 = jnp.float32

    def bound(kernel, *values):
        return lambda *refs: kernel(*values, *refs)

    blocks = atoms // LANES
    total = nx * ny * nz
    dma = pltpu.SemaphoreType.DMA
    return pl.pallas_call(
        bound(step_kernel, sizes),
        name="step",
        out_shape=(
            jax.ShapeDtypeStruct(fraction.shape, f32),
            jax.ShapeDtypeStruct((1,), f32),
            jax.ShapeDtypeStruct((1,), f32),
        ),
        in_specs=[smem] * 7 + [vmem] * 4,
        out_specs=(vmem, smem, smem),
        scratch_shapes=[
            pltpu.VMEM((slots, 5, 1, atoms), f32),
            pltpu.VMEM((8, 2 * mig), f32),
            pltpu.VMEM((2, 8, 2 * mig), f32),
            pltpu.VMEM((blocks, 7, LANES, LANES), f32),
            pltpu.VMEM((blocks, 3, LANES, LANES), f32),
            pltpu.VMEM((slots * blocks, 8, LANES), f32),
            pltpu.VMEM((3, 8, LANES), f32),
            pltpu.VMEM((8, LANES), f32),
            pltpu.VMEM((total, 8, LANES), f32),
            dma((2,)),
            dma((2,)),
            dma((slots,)),
            dma((slots,)),
            dma((total,)),
            dma((total,)),
        ],
        compiler_params=pltpu.CompilerParams(collective_id=0, has_side_effects=True),
    )(
        domain_edge,
        coupling,
        sigma_table,
        depth_table,
        charge_table,
        neighbours.reshape(blocks, 1, -1),
        counts,
        fraction,
        atom_type,
        perturbed,
        leaving,
    )


def solution(mesh):
    sizes = (mesh.shape["dx"], mesh.shape["dy"], mesh.shape["dz"])
    return jax.shard_map(
        lambda *arrays: on_device(sizes, *arrays),
        mesh=mesh,
        in_specs=(
            P(None, ("win", "dx"), "dy", "dz", None),
            P(("win", "dx"), "dy", "dz", None),
            P(("win", "dx"), "dy", "dz", None),
            P(("win", "dx"), "dy", "dz", None, None),
            P(("win", "dx"), "dy", "dz", None, None),
            P(("win", "dx"), "dy", "dz", None),
            P(),
            P(),
            P(),
            P(),
            P("win"),
        ),
        out_specs=(P(None, ("win", "dx"), "dy", "dz", None), P("win"), P("win")),
        check_vma=False,
    )
```

time: 43.6 us -> 40.6 us (0.931)
  Pallas kernels: 38.7 us -> 34.2 us
  local copies, waits for them, and re-layouts: 0 us -> 1.3 us
    pallas_call x3 -> x1, Pallas kernels: 38.7 us -> 34.2 us  [on_device(): pl.pallas_call(bound(step_kernel, sizes), name='step', out_shape=(jax.Sha...]
    unnamed x0 -> x1, local copies, waits for them, and re-layouts: none -> 1.3 us
where the time goes in v3:
time: 40.6 us; the launch traced here: 40.3 us
  Pallas kernels  34.2 us (84%)
  between operations  4.81 us (12%)
  local copies, waits for them, and re-layouts  1.3 us (3%)
    pallas_call x1, Pallas kernels, on_device(): pl.pallas_call(bound(step_kernel, sizes), name='step', out_shape=(jax.Sha...  34.2 us
    unnamed x1, local copies, waits for them, and re-layouts  1.3 us

profile of v3, /device:TPU:0, one launch (start us, length us, event | category | flops | bytes accessed | tf_op | source)
XLA Modules:
  0.0 40.3 jit_solution(2718019046264153092)
XLA Ops:
  1.3 34.2 %step.1 = (f32[3,1,1,1,768]{4,3,2,1,0:T(1,128)}, f32[1]{0:T(128)}, f32[1]{0:T(128)}) custom-call(f32[3]{0:T(128)} %refs_0_.1, f32[1]{0:T(128)S(6)} %copy.17.refs_1_, f32[32]{0:T(128)} %refs_2_.1, f32[32]{0:T(128)} %refs_3_.1, f32[32]{0:T(128)} %refs_4_.1, s32[6,1,16]{2,1,0:T(1,128)} %bitcast.1, s32[1,1,1,6]{3,2,1,0:T(1,128)} %refs_6_.1, ...), custom_call_target="tpu_custom_call" | custom-call | tf_op jit(solution)/shard_map/step/pallas_call | solution.py:364
  35.5 1.3 %copy.18 = f32[3,1,1,1,768]{4,3,2,1,0:T(1,128)} copy(f32[3,1,1,1,768]{4,3,2,1,0:T(1,128)} %get-tuple-element.6) | data formatting | bytes 18432

commit v4 on v3

--- a/solution.py
+++ b/solution.py
@@ -294,7 +294,7 @@
             sums_ref[2] += tot_k
 
         width = listed_ref.shape[-1]
-        unroll = 2 if width % 2 == 0 else 1
+        unroll = 4 if width % 4 == 0 else 1
 
         @pl.loop(0, width // unroll)
         def _(step):

time: 40.6 us -> 39.7 us (0.978)
  Pallas kernels: 34.2 us -> 33.4 us
    pallas_call x1, Pallas kernels: 34.2 us -> 33.4 us  [on_device(): pl.pallas_call(bound(step_kernel, sizes), name='step', out_shape=(jax.Sha...]
where the time goes in v4:
time: 39.7 us; the launch traced here: 39.5 us
  Pallas kernels  33.4 us (84%)
  between operations  4.81 us (12%)
  local copies, waits for them, and re-layouts  1.3 us (3%)
    pallas_call x1, Pallas kernels, on_device(): pl.pallas_call(bound(step_kernel, sizes), name='step', out_shape=(jax.Sha...  33.4 us
    unnamed x1, local copies, waits for them, and re-layouts  1.3 us

profile of v4, /device:TPU:0, one launch (start us, length us, event | category | flops | bytes accessed | tf_op | source)
XLA Modules:
  0.0 39.5 jit_solution(9392003931020881873)
XLA Ops:
  1.3 33.4 %step.1 = (f32[3,1,1,1,768]{4,3,2,1,0:T(1,128)}, f32[1]{0:T(128)}, f32[1]{0:T(128)}) custom-call(f32[3]{0:T(128)} %refs_0_.1, f32[1]{0:T(128)S(6)} %copy.17.refs_1_, f32[32]{0:T(128)} %refs_2_.1, f32[32]{0:T(128)} %refs_3_.1, f32[32]{0:T(128)} %refs_4_.1, s32[6,1,16]{2,1,0:T(1,128)} %bitcast.1, s32[1,1,1,6]{3,2,1,0:T(1,128)} %refs_6_.1, ...), custom_call_target="tpu_custom_call" | custom-call | tf_op jit(solution)/shard_map/step/pallas_call | solution.py:364
  34.7 1.3 %copy.18 = f32[3,1,1,1,768]{4,3,2,1,0:T(1,128)} copy(f32[3,1,1,1,768]{4,3,2,1,0:T(1,128)} %get-tuple-element.6) | data formatting | bytes 18432
